TPU v7x, 32 devices: a whole 2x2x4 slice. The times are simulated.
32 devices in a mesh: zero: 4 (over y, x), width: 2 (over core), site: 4 (over z).
Axes of the slice: x: 2, y: 2, z: 4, core: 2. Of those that a mesh axis runs over, the one named last changes fastest.
Arguments:
- train_query: bfloat16 [28672, 7168], P(('site', 'zero'), 'width'), parts along dimension 0, may hold values from -0.09375 to 0.09375
- low_query: bfloat16 [28672, 64], P(('site', 'zero')), parts along dimension 0, may hold values from -0.0625 to 0.0625
- high_query: bfloat16 [256, 7168], P('site', 'width'), parts along dimension 0, may hold values from -0.75 to 0.75
- train_key: bfloat16 [28672, 7168], P(('site', 'zero'), 'width'), parts along dimension 0, may hold values from -0.09375 to 0.09375
- low_key: bfloat16 [28672, 64], P(('site', 'zero')), parts along dimension 0, may hold values from -0.0625 to 0.0625
- high_key: bfloat16 [256, 7168], P('site', 'width'), parts along dimension 0, may hold values from -0.75 to 0.75
- train_value: bfloat16 [28672, 7168], P(('site', 'zero'), 'width'), parts along dimension 0, may hold values from -0.09375 to 0.09375
- low_value: bfloat16 [28672, 64], P(('site', 'zero')), parts along dimension 0, may hold values from -0.0625 to 0.0625
- high_value: bfloat16 [256, 7168], P('site', 'width'), parts along dimension 0, may hold values from -0.75 to 0.75
- norm_train: float32 [28672], P(('site', 'zero', 'width')), parts along dimension 0, may hold values from 0.25 to 1.75
- norm_step: float32 [28672], P(('site', 'zero', 'width')), parts along dimension 0, may hold values from -0.3 to 0.3
Outputs:
- final_query: bfloat16 [28672, 7168], P('site', ('width', 'zero')), parts along dimension 0
- final_key: bfloat16 [28672, 7168], P('site', ('width', 'zero')), parts along dimension 0
- final_value: bfloat16 [28672, 7168], P('site', ('width', 'zero')), parts along dimension 0
- scale_query: float32 [28672], P(('site', 'width', 'zero')), parts along dimension 0
- scale_key: float32 [28672], P(('site', 'width', 'zero')), parts along dimension 0
- scale_value: float32 [28672], P(('site', 'width', 'zero')), parts along dimension 0
- serve_norm: bfloat16 [28672], P('site'), parts along dimension 0
There are 4 independent parts, one for each index of `site`. A program takes and returns all parts, laid end to end along the dimension named above; each array names one. Nothing has to cross between parts.
All inputs are finite; a program needn't handle non-finite values. Where the computation divides by a largest or mean magnitude, that divisor is 1e-20 or more.
Results may differ from a plain program's by a relative error of at most 0.01.
Values may be sent and summed in bfloat16 or wider, within the bound.
A program may use at most 256 MiB of HBM per device.

v0:
```python
import jax
import jax.numpy as jnp
from jax import lax
from jax.sharding import PartitionSpec as P

D_MODEL = 7168


mix_rate = 1.0


def shards(
    train_query,
    low_query,
    high_query,
    train_key,
    low_key,
    high_key,
    train_value,
    low_value,
    high_value,
    norm_train,
    norm_step,
):
    result_query = train_query.astype(jnp.float32) + mix_rate * jnp.dot(
        low_query, high_query, preferred_element_type=jnp.float32
    )
    result_key = train_key.astype(jnp.float32) + mix_rate * jnp.dot(
        low_key, high_key, preferred_element_type=jnp.float32
    )
    result_value = train_value.astype(jnp.float32) + mix_rate * jnp.dot(
        low_value, high_value, preferred_element_type=jnp.float32
    )
    total_query, total_key, total_value = (
        lax.psum(jnp.sum(jnp.abs(result_query), axis=0).astype(jnp.bfloat16), "zero").astype(
            jnp.float32
        ),
        lax.psum(jnp.sum(jnp.abs(result_key), axis=0).astype(jnp.bfloat16), "zero").astype(
            jnp.float32
        ),
        lax.psum(jnp.sum(jnp.abs(result_value), axis=0).astype(jnp.bfloat16), "zero").astype(
            jnp.float32
        ),
    )
    scale_query = total_query / D_MODEL
    scale_key = total_key / D_MODEL
    scale_value = total_value / D_MODEL
    narrow_query, narrow_key, narrow_value = (
        (result_query / scale_query).astype(jnp.bfloat16),
        (result_key / scale_key).astype(jnp.bfloat16),
        (result_value / scale_value).astype(jnp.bfloat16),
    )
    final_query, final_key, final_value = (
        lax.all_to_all(narrow_query, "zero", split_axis=1, concat_axis=0, tiled=True),
        lax.all_to_all(narrow_key, "zero", split_axis=1, concat_axis=0, tiled=True),
        lax.all_to_all(narrow_value, "zero", split_axis=1, concat_axis=0, tiled=True),
    )
    place = lax.axis_index("zero")
    scale_query = lax.dynamic_slice_in_dim(
        scale_query, place * final_query.shape[1], final_query.shape[1]
    )
    scale_key = lax.dynamic_slice_in_dim(scale_key, place * final_key.shape[1], final_key.shape[1])
    scale_value = lax.dynamic_slice_in_dim(
        scale_value, place * final_value.shape[1], final_value.shape[1]
    )
    serve_norm = lax.all_gather(
        (norm_train + norm_step).astype(jnp.bfloat16), ("zero", "width"), axis=0, tiled=True
    )
    return (final_query, final_key, final_value, scale_query, scale_key, scale_value, serve_norm)


def solution(mesh):
    in_specs = (
        P(("site", "zero"), "width"),
        P(("site", "zero"), None),
        P("site", "width"),
        P(("site", "zero"), "width"),
        P(("site", "zero"), None),
        P("site", "width"),
        P(("site", "zero"), "width"),
        P(("site", "zero"), None),
        P("site", "width"),
        P(("site", "zero", "width")),
        P(("site", "zero", "width")),
    )
    out_specs = (
        P("site", ("width", "zero")),
        P("site", ("width", "zero")),
        P("site", ("width", "zero")),
        P(("site", "width", "zero")),
        P(("site", "width", "zero")),
        P(("site", "width", "zero")),
        P("site"),
    )
    return jax.shard_map(shards, mesh=mesh, in_specs=in_specs, out_specs=out_specs, check_vma=False)
```

profile of v0, /device:TPU:0, one launch (start us, length us, event | category | flops | bytes accessed | tf_op | source)
XLA Modules:
  0.0 547.0 jit_solution(10989158017610748947)
XLA Ops:
  0.6 0.0 copy-start
  0.7 0.0 copy-start.2
  0.7 0.0 copy-start.5
  0.7 0.0 copy-start.3
  0.7 1.0 copy-done
  1.7 15.1 %abs_reduce_fusion.2 = (bf16[3584]{0:T(1024)(128)(2,1)S(1)}, f32[1792,3584]{1,0:T(8,128)}) fusion(bf16[1792,3584]{1,0:T(8,128)(2,1)} %param.11, bf16[1792,64]{0,1:T(8,128)(2,1)} %param.12, bf16[64,3584]{1,0:T(8,128)(2,1)S(1)} %copy-done), kind=kOutput, calls=%fused_computation.7 | convolution fusion | flops 847770112 | bytes 39230464 | tf_op jit(solution)/shard_map/dot_general | solution.py:25
  16.8 0.0 copy-done.2
  16.8 0.0 copy-done.5
  16.8 0.0 copy-done.3
  16.8 0.0 copy-start.4
  16.8 0.0 copy-start.6
  16.8 10.5 %abs_reduce_fusion.1 = (bf16[3584]{0:T(1024)(128)(2,1)S(1)}, f32[1792,3584]{1,0:T(8,128)}) fusion(bf16[1792,3584]{1,0:T(8,128)(2,1)S(1)} %copy-done.2, bf16[1792,64]{0,1:T(8,128)(2,1)S(1)} %copy-done.5, bf16[64,3584]{1,0:T(8,128)(2,1)S(1)} %copy-done.3), kind=kOutput, calls=%fused_computation.4 | convolution fusion | flops 847770112 | bytes 39230464 | tf_op jit(solution)/shard_map/dot_general | solution.py:28
  27.4 0.0 copy-done.4
  27.4 0.0 copy-done.6
  27.4 13.4 %abs_reduce_fusion = (bf16[3584]{0:T(1024)(128)(2,1)S(1)}, f32[1792,3584]{1,0:T(8,128)}) fusion(bf16[1792,3584]{1,0:T(8,128)(2,1)} %param.17, bf16[1792,64]{0,1:T(8,128)(2,1)S(1)} %copy-done.6, bf16[64,3584]{1,0:T(8,128)(2,1)S(1)} %copy-done.4), kind=kOutput, calls=%fused_computation.1 | convolution fusion | flops 847770112 | bytes 39230464 | tf_op jit(solution)/shard_map/dot_general | solution.py:31
  40.8 17.7 %all-reduce = (bf16[3584]{0:T(1024)(128)(2,1)S(1)}, bf16[3584]{0:T(1024)(128)(2,1)S(1)}, bf16[3584]{0:T(1024)(128)(2,1)S(1)}) all-reduce(bf16[3584]{0:T(1024)(128)(2,1)S(1)} %get-tuple-element.10, bf16[3584]{0:T(1024)(128)(2,1)S(1)} %get-tuple-element.12, ...), channel_id=1, replica_groups=mesh['zero'=4,'width'=2,'site'=4] {'zero'}, use_global_device_ids=true, to_apply=%region_1.0 | all-reduce | flops 10752 | bytes 43008 | tf_op jit(solution)/shard_map/psum | solution.py:35
  58.5 12.8 %divide_convert_fusion.2 = bf16[1792,3584]{1,0:T(8,128)(2,1)S(1)} fusion(f32[1792,3584]{1,0:T(8,128)} %get-tuple-element.11, bf16[1792,3584]{1,0:T(8,128)(2,1)} %param.11, f32[3584]{0:T(1024)S(1)} %convert_multiply_fusion.2), kind=kLoop, calls=%fused_computation.6 | loop fusion | flops 25690112 | bytes 51394560 | tf_op jit(solution)/shard_map/convert_element_type | solution.py:49
  71.3 5.3 copy.35
  76.6 6.5 %all-to-all-start = ((bf16[1792,4,896]{2,0,1:T(8,128)(2,1)}), bf16[1792,4,896]{2,0,1:T(8,128)(2,1)}, u32[]{:S(2)}, u32[]{:S(2)}) async-start(bf16[1792,4,896]{2,0,1:T(8,128)(2,1)} %bitcast.29), calls=%async_computation | async-start | bytes 25690112 | tf_op jit(solution)/shard_map/all_to_all | solution.py:54
  83.1 12.8 %divide_convert_fusion.1 = bf16[1792,3584]{1,0:T(8,128)(2,1)S(1)} fusion(f32[1792,3584]{1,0:T(8,128)} %get-tuple-element.13, bf16[1792,3584]{1,0:T(8,128)(2,1)} %param.14, f32[3584]{0:T(1024)S(1)} %convert_multiply_fusion.1), kind=kLoop, calls=%fused_computation.3 | loop fusion | flops 25690112 | bytes 51394560 | tf_op jit(solution)/shard_map/convert_element_type | solution.py:50
  95.9 5.3 copy.34
  101.2 118.5 %all-to-all-done = bf16[1792,4,896]{2,0,1:T(8,128)(2,1)} async-done(((bf16[1792,4,896]{2,0,1:T(8,128)(2,1)}), bf16[1792,4,896]{2,0,1:T(8,128)(2,1)}, u32[]{:S(2)}, u32[]{:S(2)}) %all-to-all-start) | async-done | bytes 12845088 | tf_op jit(solution)/shard_map/all_to_all | solution.py:54
  219.7 6.3 %all-to-all-start.1 = ((bf16[1792,4,896]{2,0,1:T(8,128)(2,1)}), bf16[1792,4,896]{2,0,1:T(8,128)(2,1)}, u32[]{:S(2)}, u32[]{:S(2)}) async-start(bf16[1792,4,896]{2,0,1:T(8,128)(2,1)} %bitcast.28), calls=%async_computation.1 | async-start | bytes 25690112 | tf_op jit(solution)/shard_map/all_to_all | solution.py:55
  226.0 12.8 %divide_convert_fusion = bf16[1792,3584]{1,0:T(8,128)(2,1)S(1)} fusion(f32[1792,3584]{1,0:T(8,128)} %get-tuple-element.15, bf16[1792,3584]{1,0:T(8,128)(2,1)} %param.17, f32[3584]{0:T(1024)S(1)} %convert_multiply_fusion), kind=kLoop, calls=%fused_computation | loop fusion | flops 25690112 | bytes 51394560 | tf_op jit(solution)/shard_map/convert_element_type | solution.py:51
  238.9 0.0 copy-start.7
  238.9 0.0 copy-start.8
  238.9 5.3 copy.33
  244.2 121.5 %all-to-all-done.1 = bf16[1792,4,896]{2,0,1:T(8,128)(2,1)} async-done(((bf16[1792,4,896]{2,0,1:T(8,128)(2,1)}), bf16[1792,4,896]{2,0,1:T(8,128)(2,1)}, u32[]{:S(2)}, u32[]{:S(2)}) %all-to-all-start.1) | async-done | bytes 12845088 | tf_op jit(solution)/shard_map/all_to_all | solution.py:55
  365.6 6.3 %all-to-all-start.2 = ((bf16[1792,4,896]{2,0,1:T(8,128)(2,1)}), bf16[1792,4,896]{2,0,1:T(8,128)(2,1)}, u32[]{:S(2)}, u32[]{:S(2)}) async-start(bf16[1792,4,896]{2,0,1:T(8,128)(2,1)} %bitcast.27), calls=%async_computation.2 | async-start | bytes 25690112 | tf_op jit(solution)/shard_map/all_to_all | solution.py:56
  372.0 0.7 dynamic_slice.9
  372.6 0.7 dynamic_slice.10
  373.3 0.7 dynamic_slice.11
  374.0 0.0 copy-done.7
  374.0 0.0 copy-done.8
  374.0 140.2 %all-gather = bf16[8,1,896]{2,1,0:T(2,128)(2,1)S(1)} all-gather(bf16[1,1,896]{2,1,0:T(2,128)(2,1)S(1)} %reshape.26), channel_id=1, replica_groups=mesh['zero'=4,'width'=2,'site'=4] {'zero','width'}, dimensions={0}, use_global_device_ids=true | all-gather | bytes 16128 | tf_op jit(solution)/shard_map/all_gather | solution.py:66
  514.2 0.1 reduce
  514.2 0.6 reshape.27
  514.9 0.0 all-to-all-done.2
  514.9 0.0 copy-start.1
  514.9 10.7 %copy.39 = bf16[7168,896]{1,0:T(8,128)(2,1)} copy(bf16[7168,896]{1,0:T(8,128)(2,1)} %bitcast.1) | data formatting | bytes 25690112
  525.6 10.7 %copy.40 = bf16[7168,896]{1,0:T(8,128)(2,1)} copy(bf16[7168,896]{1,0:T(8,128)(2,1)} %bitcast.3) | data formatting | bytes 25690112
  536.3 10.7 %copy.41 = bf16[7168,896]{1,0:T(8,128)(2,1)} copy(bf16[7168,896]{1,0:T(8,128)(2,1)} %bitcast.5) | data formatting | bytes 25690112
  547.0 0.0 copy-done.1
  (5 shorter events, 0.0 us)
Async XLA Ops:
  0.6 1.0 copy-start
  0.7 16.1 %copy-start.2 = (bf16[1792,3584]{1,0:T(8,128)(2,1)S(1)}, bf16[1792,3584]{1,0:T(8,128)(2,1)}, u32[]{:S(2)}) copy-start(bf16[1792,3584]{1,0:T(8,128)(2,1)} %param.14) | copy-start | bytes 38535172
  0.7 16.1 %copy-start.5 = (bf16[1792,64]{0,1:T(8,128)(2,1)S(1)}, bf16[1792,64]{0,1:T(8,128)(2,1)}, u32[]{:S(2)}) copy-start(bf16[1792,64]{0,1:T(8,128)(2,1)} %param.15) | copy-start | bytes 688132
  0.7 16.1 %copy-start.3 = (bf16[64,3584]{1,0:T(8,128)(2,1)S(1)}, bf16[64,3584]{1,0:T(8,128)(2,1)}, u32[]{:S(2)}) copy-start(bf16[64,3584]{1,0:T(8,128)(2,1)} %param.16) | copy-start | bytes 1376260
  16.8 10.6 %copy-start.4 = (bf16[64,3584]{1,0:T(8,128)(2,1)S(1)}, bf16[64,3584]{1,0:T(8,128)(2,1)}, u32[]{:S(2)}) copy-start(bf16[64,3584]{1,0:T(8,128)(2,1)} %param.19) | copy-start | bytes 1376260
  16.8 10.6 %copy-start.6 = (bf16[1792,64]{0,1:T(8,128)(2,1)S(1)}, bf16[1792,64]{0,1:T(8,128)(2,1)}, u32[]{:S(2)}) copy-start(bf16[1792,64]{0,1:T(8,128)(2,1)} %param.18) | copy-start | bytes 688132
  76.6 143.1 %all-to-all-start = ((bf16[1792,4,896]{2,0,1:T(8,128)(2,1)}), bf16[1792,4,896]{2,0,1:T(8,128)(2,1)}, u32[]{:S(2)}, u32[]{:S(2)}) async-start(bf16[1792,4,896]{2,0,1:T(8,128)(2,1)} %bitcast.29), calls=%async_computation | async-start | bytes 25690112 | tf_op jit(solution)/shard_map/all_to_all | solution.py:54
  219.7 146.0 %all-to-all-start.1 = ((bf16[1792,4,896]{2,0,1:T(8,128)(2,1)}), bf16[1792,4,896]{2,0,1:T(8,128)(2,1)}, u32[]{:S(2)}, u32[]{:S(2)}) async-start(bf16[1792,4,896]{2,0,1:T(8,128)(2,1)} %bitcast.28), calls=%async_computation.1 | async-start | bytes 25690112 | tf_op jit(solution)/shard_map/all_to_all | solution.py:55
  238.9 135.1 %copy-start.7 = (f32[896]{0:T(1024)S(1)}, f32[896]{0:T(1024)}, u32[]{:S(2)}) copy-start(f32[896]{0:T(1024)} %param.20) | copy-start | bytes 10756
  238.9 135.1 %copy-start.8 = (f32[896]{0:T(1024)S(1)}, f32[896]{0:T(1024)}, u32[]{:S(2)}) copy-start(f32[896]{0:T(1024)} %param.21) | copy-start | bytes 10756
  365.6 149.3 %all-to-all-start.2 = ((bf16[1792,4,896]{2,0,1:T(8,128)(2,1)}), bf16[1792,4,896]{2,0,1:T(8,128)(2,1)}, u32[]{:S(2)}, u32[]{:S(2)}) async-start(bf16[1792,4,896]{2,0,1:T(8,128)(2,1)} %bitcast.27), calls=%async_computation.2 | async-start | bytes 25690112 | tf_op jit(solution)/shard_map/all_to_all | solution.py:56
  514.9 32.1 %copy-start.1 = (bf16[64,3584]{1,0:T(8,128)(2,1)S(1)}, bf16[64,3584]{1,0:T(8,128)(2,1)}, u32[]{:S(2)}) copy-start(bf16[64,3584]{1,0:T(8,128)(2,1)} %param.13) | copy-start | bytes 1376260
where the time goes:
time: 548 us; the launch traced here: 547 us
  waiting for transfers between devices  240 us (44%)
  blocking collectives  158 us (29%)
  local copies, waits for them, and re-layouts  51.6 us (9%)
  matrix products  39.1 us (7%)
  other arithmetic  38.6 us (7%)
  starting transfers between devices  19.1 us (3%)
    all_gather x1, blocking collectives, shards(): lax.all_gather((norm_train + norm_step).astype(jnp.bfloat16), ('zero', 'w...  140 us
    all_to_all x1, waiting for transfers between devices, shards(): lax.all_to_all(narrow_key, 'zero', split_axis=1, concat_axis=0, tiled=True)  121 us
    all_to_all x1, waiting for transfers between devices, shards(): lax.all_to_all(narrow_query, 'zero', split_axis=1, concat_axis=0, tiled=T...  118 us
    unnamed x23, local copies, waits for them, and re-layouts  33.8 us
    psum x1, blocking collectives, shards(): lax.psum(jnp.sum(jnp.abs(result_query), axis=0).astype(jnp.bfloat16), 'ze...  17.7 us
    dot_general x1, matrix products, shards(): jnp.dot(low_query, high_query, preferred_element_type=jnp.float32)  15.1 us
    dot_general x1, matrix products, shards(): jnp.dot(low_value, high_value, preferred_element_type=jnp.float32)  13.4 us
    convert_element_type x1, other arithmetic, shards(): (result_query / scale_query).astype(jnp.bfloat16)  12.8 us
  transfers between devices with their start and end apart: 3, of which 2 were waited for; matrix products, arithmetic and copies ran while one was open for 7% of the time, Pallas kernels for 0%

commit v1 on v0

v1 whole, which is shorter than its diff:
```python
import functools

import jax
import jax.numpy as jnp
from jax import lax
from jax.experimental import pallas as pl
from jax.experimental.pallas import tpu as pltpu
from jax.sharding import PartitionSpec as P


mix_rate = 1.0
LANES = 128
CUTS = ((1,), (), (-1,))


def merged(train, low, high):
    product = jnp.dot(low, high, preferred_element_type=jnp.float32)
    return (train.astype(jnp.float32) + mix_rate * product).astype(jnp.bfloat16)


def finish_body(peers, tiles, step, offset, extra, *refs):
    blocks, rest = refs[:peers], refs[peers + extra :]
    out_ref, scale_ref, held, in_sem, out_sem = rest
    rows, columns = blocks[0].shape
    tile = rows // tiles
    me = lax.axis_index("zero")

    def fetch(m, t):
        span = pl.ds(t * tile, tile)
        return pltpu.make_async_copy(blocks[m].at[span], held.at[m, span], in_sem.at[m, t])

    def put(m, t):
        span = pl.ds(t * tile, tile)
        place = pl.multiple_of((me ^ m) * rows + t * tile, 16)
        target = out_ref.at[pl.ds(place, tile), pl.ds(offset, columns)]
        return pltpu.make_async_copy(held.at[m, span], target, out_sem.at[m, t])

    for m in range(peers):
        for t in range(tiles):
            fetch(m, t).start()
    total = jnp.zeros((8, columns), jnp.float32)
    for m in range(peers):
        for t in range(tiles):
            fetch(m, t).wait()

            def add(i, acc, m=m, t=t):
                base = pl.multiple_of(t * tile + i * step, step)
                size = jnp.abs(held[m, pl.ds(base, step), :].astype(jnp.float32))
                while size.shape[0] > 8:
                    half = size.shape[0] // 2
                    size = size[:half] + size[half:]
                return acc + size

            total = lax.fori_loop(0, tile // step, add, total)
    scale = jnp.sum(total, axis=0, keepdims=True) / (rows * peers)
    scale_ref[...] = scale
    inverse = 1.0 / scale
    for m in range(peers):
        for t in range(tiles):

            def divide(i, carry, m=m, t=t):
                base = pl.multiple_of(t * tile + i * step, step)
                span = pl.ds(base, step)
                held[m, span, :] = (held[m, span, :].astype(jnp.float32) * inverse).astype(
                    jnp.bfloat16
                )
                return carry

            lax.fori_loop(0, tile // step, divide, 0)
            put(m, t).start()
    for m in range(peers):
        for t in range(tiles):
            put(m, t).wait()


def finish(blocks, previous, after, offset, width):
    peers = len(blocks)
    rows, columns = blocks[0].shape
    tiles = 7 if rows % (7 * 32) == 0 else 1
    tile = rows // tiles
    step = max(s for s in (16, 32, 64, 128, 256) if tile % s == 0 and (s == 16 or s * columns <= 1 << 16))
    aliased = previous is not None
    operands = list(blocks) + ([previous] if aliased else []) + ([] if after is None else [after])
    size = 2 * rows * peers * columns
    return pl.pallas_call(
        functools.partial(finish_body, peers, tiles, step, offset, len(operands) - peers),
        out_shape=(
            jax.ShapeDtypeStruct((rows * peers, width), jnp.bfloat16),
            jax.ShapeDtypeStruct((1, columns), jnp.float32),
        ),
        in_specs=[pl.BlockSpec(memory_space=pl.ANY)] * len(operands),
        out_specs=(pl.BlockSpec(memory_space=pl.ANY), pl.BlockSpec(memory_space=pltpu.VMEM)),
        scratch_shapes=[
            pltpu.VMEM((peers, rows, columns), jnp.bfloat16),
            pltpu.SemaphoreType.DMA((peers, tiles)),
            pltpu.SemaphoreType.DMA((peers, tiles)),
        ],
        input_output_aliases={peers: 0} if aliased else {},
        compiler_params=pltpu.CompilerParams(vmem_limit_bytes=size + (4 << 20)),
        cost_estimate=pl.CostEstimate(
            flops=4 * size, bytes_accessed=2 * size, transcendentals=0
        ),
        name="finish",
    )(*operands)


def pairs(n, m):
    return [(i, i ^ m) for i in range(n)]


def cuts_of(width, inner):
    lanes = width // LANES
    return [0] + [cut % lanes * LANES for cut in inner if lanes > 1] + [width]


def project_all(triples, gain, n, w):
    me, core = lax.axis_index("zero"), lax.axis_index("width")

    def send(block, m):
        return lax.ppermute(block, "zero", pairs(n, m))

    order = sorted(range(1, n), key=lambda m: (-bin(m).count("1"), m)) + [0]
    chunks, last, gains, step = [], None, None, 0
    for index, (train, low, high) in enumerate(triples):
        width = train.shape[1] // n
        cuts = cuts_of(width, CUTS[index])
        for begin, end in zip(cuts[:-1], cuts[1:]):
            blocks = {}
            for m in order:
                if last is not None:
                    low, last = lax.optimization_barrier((low, last))
                at = (me ^ m) * width + begin
                last = merged(
                    lax.dynamic_slice_in_dim(train, at, end - begin, axis=1),
                    low,
                    lax.dynamic_slice_in_dim(high, at, end - begin, axis=1),
                )
                blocks[m] = send(last, m) if m else last
                step += 1
            chunks.append((index, begin, width, [blocks[m] for m in range(n)]))
        if gains is None:
            gain, last = lax.optimization_barrier((gain, last))
            other = lax.ppermute(gain, "width", pairs(w, 1))
            both = jnp.where(core == 0, jnp.stack([gain, other]), jnp.stack([other, gain]))
            both, last = lax.optimization_barrier((both, last))
            gains = [send(both, m) if m else both for m in range(n)]
    outs, scales, after = [None] * len(triples), [[] for _ in triples], None
    for index, begin, width, blocks in chunks:
        outs[index], after = finish(blocks, outs[index], after, begin, width)
        scales[index].append(after)
        if index == 1 and begin == 0:
            gains, after = lax.optimization_barrier((gains, after))
            gain = jnp.stack(gains)[jnp.arange(n) ^ me].reshape(-1)
    return outs, [jnp.concatenate(s, axis=1).reshape(-1) for s in scales], gain


def project_plain(train, low, high):
    result = lax.all_to_all(merged(train, low, high), "zero", split_axis=1, concat_axis=0, tiled=True)
    result = result.astype(jnp.float32)
    scale = jnp.sum(jnp.abs(result), axis=0) / result.shape[0]
    return (result / scale).astype(jnp.bfloat16), scale


def shards(n, w, tq, lq, hq, tk, lk, hk, tv, lv, hv, norm_train, norm_step):
    width = tq.shape[1] // n
    direct = n & (n - 1) == 0 and n <= 8 and w == 2
    direct = direct and width % LANES == 0 and tq.shape[0] % 16 == 0
    gain = (norm_train + norm_step).astype(jnp.bfloat16)
    triples = ((tq, lq, hq), (tk, lk, hk), (tv, lv, hv))
    if direct:
        outs, scales, serve_norm = project_all(triples, gain, n, w)
    else:
        outs, scales = zip(*(project_plain(*triple) for triple in triples))
        serve_norm = lax.all_gather(gain, ("zero", "width"), axis=0, tiled=True)
    return (*outs, *scales, serve_norm)


def solution(mesh):
    rows, whole, columns = P(("site", "zero"), "width"), P(("site", "zero"), None), P("site", "width")
    vector = P(("site", "zero", "width"))
    matrix_out, vector_out = P("site", ("width", "zero")), P(("site", "width", "zero"))
    n, w = mesh.shape["zero"], mesh.shape["width"]

    def body(*arrays):
        return shards(n, w, *arrays)

    return jax.shard_map(
        body,
        mesh=mesh,
        in_specs=(rows, whole, columns) * 3 + (vector, vector),
        out_specs=(matrix_out,) * 3 + (vector_out,) * 3 + (P("site"),),
        check_vma=False,
    )
```

time: 548 us -> 516 us (0.942)
  blocking collectives: 158 us -> 0 us
  waiting for transfers between devices: 240 us -> 375 us
  local copies, waits for them, and re-layouts: 51.6 us -> 6.66 us
  Pallas kernels: 0 us -> 37.9 us
  other arithmetic: 38.6 us -> 1.89 us
  matrix products: 39.1 us -> 63.7 us
  starting transfers between devices: 19.1 us -> 29.6 us
    ppermute x0 -> x19, waiting for transfers between devices: none -> 375 us  [the longest x18 374 us: send(): return lax.ppermute(block, 'zero', pairs(n, m))]
    all_to_all x3 -> x0, waiting for transfers between devices: 240 us -> none  [the longest x1 121 us: shards(): lax.all_to_all(narrow_key, 'zero', split_axis=1, concat_axis=0, tiled=True)]
    all_gather x1 -> x0, blocking collectives: 140 us -> none  [shards(): lax.all_gather((norm_train + norm_step).astype(jnp.bfloat16), ('zero', 'w...]
    convert_element_type x4 -> x1, other arithmetic: 38.5 us -> 0.01 us  [shards(): gain = (norm_train + norm_step).astype(jnp.bfloat16)]
    pallas_call x0 -> x5, Pallas kernels: none -> 37.9 us  [finish(): pl.pallas_call(functools.partial(finish_body, peers, tiles, step, offset,...]
    ppermute x0 -> x19, starting transfers between devices: none -> 29.6 us  [the longest x18 29.6 us: send(): return lax.ppermute(block, 'zero', pairs(n, m))]
    unnamed x23 -> x44, local copies, waits for them, and re-layouts: 33.8 us -> 5.45 us
    dot_general x3 -> x20, matrix products: 39.1 us -> 63.7 us  [merged(): product = jnp.dot(low, high, preferred_element_type=jnp.float32)]
  transfers between devices with their start and end apart: 3 -> 19, of which waited for: 2 -> 13; matrix products, arithmetic and copies ran while one was open for 7% -> 10% of each run, Pallas kernels for 0% -> 7%
where the time goes in v1:
time: 516 us
  waiting for transfers between devices  375 us (73%)
  matrix products  63.7 us (12%)
  Pallas kernels  37.9 us (7%)
  starting transfers between devices  29.6 us (6%)
  local copies, waits for them, and re-layouts  6.66 us (1%)
    ppermute x18, waiting for transfers between devices, send(): return lax.ppermute(block, 'zero', pairs(n, m))  374 us
    dot_general x20, matrix products, merged(): product = jnp.dot(low, high, preferred_element_type=jnp.float32)  63.7 us
    pallas_call x5, Pallas kernels, finish(): pl.pallas_call(functools.partial(finish_body, peers, tiles, step, offset,...  37.9 us
    ppermute x18, starting transfers between devices, send(): return lax.ppermute(block, 'zero', pairs(n, m))  29.6 us
  transfers between devices with their start and end apart: 19, of which 13 were waited for; matrix products, arithmetic and copies ran while one was open for 10% of the time, Pallas kernels for 7%

profile of v1, /device:TPU:0, one launch (start us, length us, event | category | flops | bytes accessed | tf_op | source)
XLA Modules:
  0.0 515.8 jit_solution(9781776522317710325)
XLA Ops:
  0.7 2.4 fusion.2
  3.1 2.3 fusion.3
  5.4 2.2 fusion.4
  9.1 4.4 add_convert_fusion.10
  13.4 3.9 collective-permute-start.2
  17.4 4.3 add_convert_fusion.9
  22.3 4.4 add_convert_fusion.8
  26.7 4.8 fusion
  31.5 4.8 add_convert_fusion.2
  36.3 4.7 add_convert_fusion.1
  41.0 4.6 add_convert_fusion.refs_0_
  45.7 2.4 add_convert_fusion.6
  48.1 2.5 add_convert_fusion.5
  50.6 2.4 add_convert_fusion.4
  53.1 2.0 collective-permute-start.13
  55.1 2.8 add_convert_fusion.7.refs_0_
  59.1 1.6 collective-permute-start.16
  60.7 76.0 %collective-permute-done.16 = bf16[2,896]{1,0:T(2,128)(2,1)S(1)} collective-permute-done((bf16[2,896]{1,0:T(2,128)(2,1)S(1)}, bf16[2,896]{1,0:T(2,128)(2,1)S(1)}, u32[]{:S(2)}, u32[]{:S(2)}) %collective-permute-start.16) | collective-permute-done | bytes 3616 | tf_op jit(solution)/shard_map/ppermute | solution.py:120
  137.0 58.4 %collective-permute-done.17 = bf16[2,896]{1,0:T(2,128)(2,1)S(1)} collective-permute-done((bf16[2,896]{1,0:T(2,128)(2,1)S(1)}, bf16[2,896]{1,0:T(2,128)(2,1)S(1)}, u32[]{:S(2)}, u32[]{:S(2)}) %collective-permute-start.17) | collective-permute-done | bytes 3616 | tf_op jit(solution)/shard_map/ppermute | solution.py:120
  195.4 2.6 collective-permute-start.18
  198.0 1.9 collective-permute-done.18
  199.9 1.7 collective-permute-start.4
  201.6 9.8 %collective-permute-done.4.refs_2_ = bf16[1792,128]{1,0:T(8,128)(2,1)S(1)} collective-permute-done((bf16[1792,128]{1,0:T(8,128)(2,1)}, bf16[1792,128]{1,0:T(8,128)(2,1)S(1)}, u32[]{:S(2)}, u32[]{:S(2)}) %collective-permute-start.4) | collective-permute-done | bytes 458784 | tf_op jit(solution)/shard_map/ppermute | solution.py:120
  212.2 1.7 collective-permute-start.3
  213.9 9.0 %collective-permute-done.3.refs_1_ = bf16[1792,128]{1,0:T(8,128)(2,1)S(1)} collective-permute-done((bf16[1792,128]{1,0:T(8,128)(2,1)}, bf16[1792,128]{1,0:T(8,128)(2,1)S(1)}, u32[]{:S(2)}, u32[]{:S(2)}) %collective-permute-start.3) | collective-permute-done | bytes 458784 | tf_op jit(solution)/shard_map/ppermute | solution.py:120
  223.6 2.6 collective-permute-start.5
  226.3 8.1 %collective-permute-done.5.refs_3_ = bf16[1792,128]{1,0:T(8,128)(2,1)S(1)} collective-permute-done((bf16[1792,128]{1,0:T(8,128)(2,1)}, bf16[1792,128]{1,0:T(8,128)(2,1)S(1)}, u32[]{:S(2)}, u32[]{:S(2)}) %collective-permute-start.5) | collective-permute-done | bytes 458784 | tf_op jit(solution)/shard_map/ppermute | solution.py:120
  235.2 1.7 collective-permute-start.7
  236.9 1.5 collective-permute-start.6
  238.7 1.7 collective-permute-start.12
  241.8 4.7 add_convert_fusion.3.refs_0_
  246.5 2.1 fusion.6
  248.6 2.2 fusion.7
  250.8 2.1 fusion.8
  252.9 118.4 %collective-permute-done.7.refs_2_ = bf16[1792,896]{1,0:T(8,128)(2,1)} collective-permute-done((bf16[1792,896]{1,0:T(8,128)(2,1)}, bf16[1792,896]{1,0:T(8,128)(2,1)}, u32[]{:S(2)}, u32[]{:S(2)}) %collective-permute-start.7) | collective-permute-done | bytes 3211296 | tf_op jit(solution)/shard_map/ppermute | solution.py:120
  371.4 1.7 collective-permute-start.10
  373.1 1.5 collective-permute-start.9
  374.6 3.6 collective-permute-done.8.refs_3_
  378.2 2.6 collective-permute-start.11
  380.8 2.1 fusion.9.refs_0_
  386.0 4.5 finish.5
  390.6 9.4 %finish.6 = (bf16[7168,896]{1,0:T(8,128)(2,1)}, f32[1,768]{1,0:T(1,128)S(1)}) custom-call(bf16[1792,768]{1,0:T(8,128)(2,1)S(1)} %add_convert_fusion.7.refs_0_, bf16[1792,768]{1,0:T(8,128)(2,1)} %collective-permute-done.refs_1_, bf16[1792,768]{1,0:T(8,128)(2,1)} %collective-permute-done.1.refs_2_, ...), custom_call_target="tpu_custom_call", output_to_operand_aliasing={{0}: (4, {})} | custom-call | flops 44040192 | bytes 22020096 | tf_op jit(solution)/shard_map/finish/pallas_call | solution.py:85
  400.6 10.9 %finish.7 = (bf16[7168,896]{1,0:T(8,128)(2,1)}, f32[1,896]{1,0:T(1,128)S(1)}) custom-call(bf16[1792,896]{1,0:T(8,128)(2,1)S(1)} %copy-done.2, bf16[1792,896]{1,0:T(8,128)(2,1)} %collective-permute-done.6.refs_1_, bf16[1792,896]{1,0:T(8,128)(2,1)} %collective-permute-done.7.refs_2_, bf16[1792,896]{1,0:T(8,128)(2,1)} %collective-permute-done.8.refs_3_, ...), custom_call_target="tpu_custom_call" | custom-call | flops 51380224 | bytes 25690112 | tf_op jit(solution)/shard_map/finish/pallas_call | solution.py:85
  412.8 24.6 %collective-permute-done.12.refs_1_ = bf16[1792,768]{1,0:T(8,128)(2,1)} collective-permute-done((bf16[1792,768]{1,0:T(8,128)(2,1)}, bf16[1792,768]{1,0:T(8,128)(2,1)}, u32[]{:S(2)}, u32[]{:S(2)}) %collective-permute-start.12) | collective-permute-done | bytes 2752544 | tf_op jit(solution)/shard_map/ppermute | solution.py:120
  437.4 58.7 %collective-permute-done.14.refs_3_ = bf16[1792,768]{1,0:T(8,128)(2,1)} collective-permute-done((bf16[1792,768]{1,0:T(8,128)(2,1)}, bf16[1792,768]{1,0:T(8,128)(2,1)}, u32[]{:S(2)}, u32[]{:S(2)}) %collective-permute-start.14) | collective-permute-done | bytes 2752544 | tf_op jit(solution)/shard_map/ppermute | solution.py:120
  496.2 9.4 %finish.8 = (bf16[7168,896]{1,0:T(8,128)(2,1)}, f32[1,768]{1,0:T(1,128)S(1)}) custom-call(bf16[1792,768]{1,0:T(8,128)(2,1)S(1)} %copy-done.3, bf16[1792,768]{1,0:T(8,128)(2,1)} %collective-permute-done.12.refs_1_, bf16[1792,768]{1,0:T(8,128)(2,1)} %collective-permute-done.13.refs_2_, bf16[1792,768]{1,0:T(8,128)(2,1)} %collective-permute-done.14.refs_3_, ...), custom_call_target="tpu_custom_call" | custom-call | flops 44040192 | bytes 22020096 | tf_op jit(solution)/shard_map/finish/pallas_call | solution.py:85
  506.2 4.7 collective-permute-done.11.refs_3_
  510.9 3.7 finish.9
  (72 shorter events, 14.6 us)
Async XLA Ops:
  0.6 26.1 %copy-start = (bf16[64,3584]{1,0:T(8,128)(2,1)S(1)}, bf16[64,3584]{1,0:T(8,128)(2,1)}, u32[]{:S(2)}) copy-start(bf16[64,3584]{1,0:T(8,128)(2,1)} %param.16) | copy-start | bytes 1376260
  0.6 16.7 %copy-start.11 = (bf16[1792,64]{0,1:T(8,128)(2,1)S(1)}, bf16[1792,64]{0,1:T(8,128)(2,1)}, u32[]{:S(2)}) copy-start(bf16[1792,64]{0,1:T(8,128)(2,1)} %param.12) | copy-start | bytes 688132
  13.4 225.2 %collective-permute-start.2 = (bf16[1792,768]{1,0:T(8,128)(2,1)}, bf16[1792,768]{1,0:T(8,128)(2,1)}, u32[]{:S(2)}, u32[]{:S(2)}) collective-permute-start(bf16[1792,768]{1,0:T(8,128)(2,1)} %add_convert_fusion.10), channel_id=1, source_target_pairs={{0,24},{8,16},{16,8},{24,0},{1,25},{9,17},{17,9},{25,1},{2,26},{10... | collective-permute-start | bytes 8257544 | tf_op jit(solution)/shard_map/ppermute | solution.py:120
  17.4 9.3 %copy-start.14 = (bf16[1792,64]{0,1:T(8,128)(2,1)S(1)}, bf16[1792,64]{0,1:T(8,128)(2,1)}, u32[]{:S(2)}) copy-start(bf16[1792,64]{0,1:T(8,128)(2,1)} %param.15) | copy-start | bytes 688132
  21.7 216.6 %collective-permute-start = (bf16[1792,768]{1,0:T(8,128)(2,1)}, bf16[1792,768]{1,0:T(8,128)(2,1)}, u32[]{:S(2)}, u32[]{:S(2)}) collective-permute-start(bf16[1792,768]{1,0:T(8,128)(2,1)} %add_convert_fusion.9), channel_id=1, source_target_pairs={{0,8},{8,0},{16,24},{24,16},{1,9},{9,1},{17,25},{25,17},{2,10},{10... | collective-permute-start | bytes 8257544 | tf_op jit(solution)/shard_map/ppermute | solution.py:120
  26.6 210.2 %collective-permute-start.1 = (bf16[1792,768]{1,0:T(8,128)(2,1)}, bf16[1792,768]{1,0:T(8,128)(2,1)}, u32[]{:S(2)}, u32[]{:S(2)}) collective-permute-start(bf16[1792,768]{1,0:T(8,128)(2,1)} %add_convert_fusion.8), channel_id=1, source_target_pairs={{0,16},{8,24},{16,0},{24,8},{1,17},{9,25},{17,1},{25,9},{2,18},{10... | collective-permute-start | bytes 8257544 | tf_op jit(solution)/shard_map/ppermute | solution.py:120
  26.7 18.9 %slice-start = ((s8[12845056]{0:T(1024)(128)(4,1)}), s8[4194304]{0:T(1024)(128)(4,1)S(1)}, s32[]{:S(2)}) async-start(s8[12845056]{0:T(1024)(128)(4,1)} %bitcast.36), calls=%async_computation | async-start | bytes 8388608
  26.7 18.9 %slice-start.1 = ((s8[12845056]{0:T(1024)(128)(4,1)}), s8[4194304]{0:T(1024)(128)(4,1)S(1)}, s32[]{:S(2)}) async-start(s8[12845056]{0:T(1024)(128)(4,1)} %bitcast.36), calls=%async_computation.1 | async-start | bytes 8388608
  31.5 14.1 %slice-start.2 = ((s8[12845056]{0:T(1024)(128)(4,1)}), s8[4194304]{0:T(1024)(128)(4,1)S(1)}, s32[]{:S(2)}) async-start(s8[12845056]{0:T(1024)(128)(4,1)} %bitcast.36), calls=%async_computation.2 | async-start | bytes 8388608
  36.3 9.4 %copy-start.12 = (bf16[1792,64]{0,1:T(8,128)(2,1)S(1)}, bf16[1792,64]{0,1:T(8,128)(2,1)}, u32[]{:S(2)}) copy-start(bf16[1792,64]{0,1:T(8,128)(2,1)} %param.18) | copy-start | bytes 688132
  36.3 9.4 %slice-start.3 = ((s8[12845056]{0:T(1024)(128)(4,1)}), s8[262144]{0:T(1024)(128)(4,1)S(1)}, s32[]{:S(2)}) async-start(s8[12845056]{0:T(1024)(128)(4,1)} %bitcast.36), calls=%async_computation.3 | async-start | bytes 524288
  36.3 9.4 %copy-start.15 = (bf16[64,3584]{1,0:T(8,128)(2,1)S(1)}, bf16[64,3584]{1,0:T(8,128)(2,1)}, u32[]{:S(2)}) copy-start(bf16[64,3584]{1,0:T(8,128)(2,1)} %param.19) | copy-start | bytes 1376260
  48.1 6.9 %copy-start.16 = (f32[896]{0:T(1024)S(1)}, f32[896]{0:T(1024)}, u32[]{:S(2)}) copy-start(f32[896]{0:T(1024)} %param.20) | copy-start | bytes 10756
  48.1 6.9 %copy-start.17 = (f32[896]{0:T(1024)S(1)}, f32[896]{0:T(1024)}, u32[]{:S(2)}) copy-start(f32[896]{0:T(1024)} %param.21) | copy-start | bytes 10756
  53.1 187.3 %collective-permute-start.13 = (bf16[1792,768]{1,0:T(8,128)(2,1)}, bf16[1792,768]{1,0:T(8,128)(2,1)}, u32[]{:S(2)}, u32[]{:S(2)}) collective-permute-start(bf16[1792,768]{1,0:T(8,128)(2,1)} %add_convert_fusion.4), channel_id=1, source_target_pairs={{0,16},{8,24},{16,0},{24,8},{1,17},{9,25},{17,1},{25,9},{2,18},{10... | collective-permute-start | bytes 8257544 | tf_op jit(solution)/shard_map/ppermute | solution.py:120
  57.8 188.7 %copy-start.13 = (bf16[1792,64]{0,1:T(8,128)(2,1)S(1)}, bf16[1792,64]{0,1:T(8,128)(2,1)}, u32[]{:S(2)}) copy-start(bf16[1792,64]{0,1:T(8,128)(2,1)} %param.18) | copy-start | bytes 688132
  57.8 1.2 collective-permute-start.15
  59.1 77.6 %collective-permute-start.16 = (bf16[2,896]{1,0:T(2,128)(2,1)S(1)}, bf16[2,896]{1,0:T(2,128)(2,1)S(1)}, u32[]{:S(2)}, u32[]{:S(2)}) collective-permute-start(bf16[2,896]{1,0:T(2,128)(2,1)S(1)} %broadcast_select_fusion), channel_id=1, source_target_pairs={{0,8},{8,0},{16,24},{24,16},{1,9},{9,1},{17,25},{25,17},{2,10},{10... | collective-permute-start | bytes 10760 | tf_op jit(solution)/shard_map/ppermute | solution.py:120
  136.7 58.7 %collective-permute-start.17 = (bf16[2,896]{1,0:T(2,128)(2,1)S(1)}, bf16[2,896]{1,0:T(2,128)(2,1)S(1)}, u32[]{:S(2)}, u32[]{:S(2)}) collective-permute-start(bf16[2,896]{1,0:T(2,128)(2,1)S(1)} %broadcast_select_fusion), channel_id=1, source_target_pairs={{0,16},{8,24},{16,0},{24,8},{1,17},{9,25},{17,1},{25,9},{2,18},{10... | collective-permute-start | bytes 10760 | tf_op jit(solution)/shard_map/ppermute | solution.py:120
  195.4 4.5 collective-permute-start.18
  199.9 11.5 %collective-permute-start.4 = (bf16[1792,128]{1,0:T(8,128)(2,1)}, bf16[1792,128]{1,0:T(8,128)(2,1)S(1)}, u32[]{:S(2)}, u32[]{:S(2)}) collective-permute-start(bf16[1792,128]{1,0:T(8,128)(2,1)} %fusion.4), channel_id=1, source_target_pairs={{0,16},{8,24},{16,0},{24,8},{1,17},{9,25},{17,1},{25,9},{2,18},{10... | collective-permute-start | bytes 1376264 | tf_op jit(solution)/shard_map/ppermute | solution.py:120
  211.4 0.8 copy-start.5
  212.2 10.7 %collective-permute-start.3 = (bf16[1792,128]{1,0:T(8,128)(2,1)}, bf16[1792,128]{1,0:T(8,128)(2,1)S(1)}, u32[]{:S(2)}, u32[]{:S(2)}) collective-permute-start(bf16[1792,128]{1,0:T(8,128)(2,1)} %fusion.3), channel_id=1, source_target_pairs={{0,8},{8,0},{16,24},{24,16},{1,9},{9,1},{17,25},{25,17},{2,10},{10... | collective-permute-start | bytes 1376264 | tf_op jit(solution)/shard_map/ppermute | solution.py:120
  222.9 0.8 copy-start.7
  223.6 10.7 %collective-permute-start.5 = (bf16[1792,128]{1,0:T(8,128)(2,1)}, bf16[1792,128]{1,0:T(8,128)(2,1)S(1)}, u32[]{:S(2)}, u32[]{:S(2)}) collective-permute-start(bf16[1792,128]{1,0:T(8,128)(2,1)} %fusion.2), channel_id=1, source_target_pairs={{0,24},{8,16},{16,8},{24,0},{1,25},{9,17},{17,9},{25,1},{2,26},{10... | collective-permute-start | bytes 1376264 | tf_op jit(solution)/shard_map/ppermute | solution.py:120
  234.4 0.8 copy-start.9
  235.2 136.2 %collective-permute-start.7 = (bf16[1792,896]{1,0:T(8,128)(2,1)}, bf16[1792,896]{1,0:T(8,128)(2,1)}, u32[]{:S(2)}, u32[]{:S(2)}) collective-permute-start(bf16[1792,896]{1,0:T(8,128)(2,1)} %add_convert_fusion.1), channel_id=1, source_target_pairs={{0,16},{8,24},{16,0},{24,8},{1,17},{9,25},{17,1},{25,9},{2,18},{10... | collective-permute-start | bytes 9633800 | tf_op jit(solution)/shard_map/ppermute | solution.py:120
  236.9 136.2 %collective-permute-start.6 = (bf16[1792,896]{1,0:T(8,128)(2,1)}, bf16[1792,896]{1,0:T(8,128)(2,1)}, u32[]{:S(2)}, u32[]{:S(2)}) collective-permute-start(bf16[1792,896]{1,0:T(8,128)(2,1)} %add_convert_fusion.2), channel_id=1, source_target_pairs={{0,8},{8,0},{16,24},{24,16},{1,9},{9,1},{17,25},{25,17},{2,10},{10... | collective-permute-start | bytes 9633800 | tf_op jit(solution)/shard_map/ppermute | solution.py:120
  238.4 139.8 %collective-permute-start.8 = (bf16[1792,896]{1,0:T(8,128)(2,1)}, bf16[1792,896]{1,0:T(8,128)(2,1)}, u32[]{:S(2)}, u32[]{:S(2)}) collective-permute-start(bf16[1792,896]{1,0:T(8,128)(2,1)} %fusion), channel_id=1, source_target_pairs={{0,24},{8,16},{16,8},{24,0},{1,25},{9,17},{17,9},{25,1},{2,26},{10... | collective-permute-start | bytes 9633800 | tf_op jit(solution)/shard_map/ppermute | solution.py:120
  238.7 198.8 %collective-permute-start.12 = (bf16[1792,768]{1,0:T(8,128)(2,1)}, bf16[1792,768]{1,0:T(8,128)(2,1)}, u32[]{:S(2)}, u32[]{:S(2)}) collective-permute-start(bf16[1792,768]{1,0:T(8,128)(2,1)} %add_convert_fusion.5), channel_id=1, source_target_pairs={{0,8},{8,0},{16,24},{24,16},{1,9},{9,1},{17,25},{25,17},{2,10},{10... | collective-permute-start | bytes 8257544 | tf_op jit(solution)/shard_map/ppermute | solution.py:120
  240.3 255.8 %collective-permute-start.14 = (bf16[1792,768]{1,0:T(8,128)(2,1)}, bf16[1792,768]{1,0:T(8,128)(2,1)}, u32[]{:S(2)}, u32[]{:S(2)}) collective-permute-start(bf16[1792,768]{1,0:T(8,128)(2,1)} %add_convert_fusion.6), channel_id=1, source_target_pairs={{0,24},{8,16},{16,8},{24,0},{1,25},{9,17},{17,9},{25,1},{2,26},{10... | collective-permute-start | bytes 8257544 | tf_op jit(solution)/shard_map/ppermute | solution.py:120
  371.4 134.2 %collective-permute-start.10 = (bf16[1792,128]{1,0:T(8,128)(2,1)}, bf16[1792,128]{1,0:T(8,128)(2,1)}, u32[]{:S(2)}, u32[]{:S(2)}) collective-permute-start(bf16[1792,128]{1,0:T(8,128)(2,1)} %fusion.8), channel_id=1, source_target_pairs={{0,16},{8,24},{16,0},{24,8},{1,17},{9,25},{17,1},{25,9},{2,18},{10... | collective-permute-start | bytes 1376264 | tf_op jit(solution)/shard_map/ppermute | solution.py:120
  373.1 133.1 %collective-permute-start.9 = (bf16[1792,128]{1,0:T(8,128)(2,1)}, bf16[1792,128]{1,0:T(8,128)(2,1)}, u32[]{:S(2)}, u32[]{:S(2)}) collective-permute-start(bf16[1792,128]{1,0:T(8,128)(2,1)} %fusion.7), channel_id=1, source_target_pairs={{0,8},{8,0},{16,24},{24,16},{1,9},{9,1},{17,25},{25,17},{2,10},{10... | collective-permute-start | bytes 1376264 | tf_op jit(solution)/shard_map/ppermute | solution.py:120
  378.2 132.7 %collective-permute-start.11 = (bf16[1792,128]{1,0:T(8,128)(2,1)}, bf16[1792,128]{1,0:T(8,128)(2,1)}, u32[]{:S(2)}, u32[]{:S(2)}) collective-permute-start(bf16[1792,128]{1,0:T(8,128)(2,1)} %fusion.6), channel_id=1, source_target_pairs={{0,24},{8,16},{16,8},{24,0},{1,25},{9,17},{17,9},{25,1},{2,26},{10... | collective-permute-start | bytes 1376264 | tf_op jit(solution)/shard_map/ppermute | solution.py:120
  383.0 1.0 copy-start.6
  384.0 1.0 copy-start.8
  385.0 1.0 copy-start.10
  390.6 10.1 %copy-start.2 = (bf16[1792,896]{1,0:T(8,128)(2,1)S(1)}, bf16[1792,896]{1,0:T(8,128)(2,1)}, u32[]{:S(2)}) copy-start(bf16[1792,896]{1,0:T(8,128)(2,1)} %add_convert_fusion.refs_0_) | copy-start | bytes 9633796
  400.6 95.5 %copy-start.3 = (bf16[1792,768]{1,0:T(8,128)(2,1)S(1)}, bf16[1792,768]{1,0:T(8,128)(2,1)}, u32[]{:S(2)}) copy-start(bf16[1792,768]{1,0:T(8,128)(2,1)} %add_convert_fusion.3.refs_0_) | copy-start | bytes 8257540
  412.8 98.1 %copy-start.4 = (bf16[1792,128]{1,0:T(8,128)(2,1)S(1)}, bf16[1792,128]{1,0:T(8,128)(2,1)}, u32[]{:S(2)}) copy-start(bf16[1792,128]{1,0:T(8,128)(2,1)} %fusion.9.refs_0_) | copy-start | bytes 1376260
  510.9 4.9 copy-start.1
